TPU v7x, 32 devices: a whole 2x2x4 slice. The times are simulated.
32 devices in a mesh: gx: 8 (over y, x, core), gy: 4 (over z).
Axes of the slice: x: 2, y: 2, z: 4, core: 2. Of those that a mesh axis runs over, the one named last changes fastest.
Arguments:
- probes: bfloat16 [256, 1024, 256], P('gx', 'gy'), may hold values from -6 to 6
- blk_rows: int32 [1024, 128], P(('gx', 'gy')), may hold values from 0 to 8191
- blk_sensor: int32 [1024], P(('gx', 'gy')), may hold values from 0 to 255, as said below
- blk_count: int32 [32], P(('gx', 'gy')), may hold values from 16 to 32, as said below
- coef: bfloat16 [1024, 128], P(('gx', 'gy')), may hold values from -5 to 5
- owner: int32 [256], replicated, may hold values from 0 to 31, as said below
- weights: float32 [256], replicated, may hold values from 0.1 to 1
Outputs:
- sensitivity: float32 [256], P(('gx', 'gy'))
- new_weights: float32 [256], replicated
- density: float32 [256, 1024], P('gx', 'gy')
Inputs may be any that keep to these rules, and one draw needn't show every extreme that they name: `owner`: every device owns exactly 8 sensors. `blk_sensor`: among the live slots of one tile, at most 2 belong to sensors of one owner; in every draw some owner receives 2 live blocks from every tile. `blk_count`: some tile has all 32 slots live.
All inputs are finite; a program needn't handle non-finite values.
Results may differ from a plain program's by a relative error of at most 0.0008.
Values may be sent and summed in bfloat16 or wider, within the bound.
A program may use at most 128 MiB of HBM per device.

v0:
```python
import jax
import jax.numpy as jnp
from jax import lax
from jax.sharding import PartitionSpec as P

SPD = 8
CAP = 2


def local(probes, blk_rows, blk_sensor, blk_count, coef, owner, weights):
    size_gx = lax.axis_size("gx")
    size_gy = lax.axis_size("gy")
    n_dev = size_gx * size_gy
    me_flat = lax.axis_index("gx") * size_gy + lax.axis_index("gy")
    tile_r, tile_c, probe_n = probes.shape
    nblk, foot = blk_rows.shape
    n_sens = owner.shape[0]
    flat = probes.reshape(tile_r * tile_c, probe_n)
    picked = flat[blk_rows.reshape(-1)].reshape(nblk, foot, probe_n)
    slots = jnp.arange(nblk, dtype=jnp.int32)
    alive = slots < blk_count[0]
    dest = owner[blk_sensor]
    earlier = (dest[:, None] == dest[None, :]) & alive[None, :] & (slots[None, :] < slots[:, None])
    rank = jnp.sum(earlier.astype(jnp.int32), axis=1)
    position = jnp.where(alive, dest * CAP + rank, n_dev * CAP)
    send_rows = (
        jnp.zeros((n_dev * CAP, foot, probe_n), jnp.bfloat16).at[position].set(picked, mode="drop")
    )
    send_coef = jnp.zeros((n_dev * CAP, foot), jnp.bfloat16).at[position].set(coef, mode="drop")
    send_ids = jnp.full((n_dev * CAP,), -1, jnp.int32).at[position].set(blk_sensor, mode="drop")
    recv_rows, recv_coef, recv_ids = (
        lax.all_to_all(send_rows, ("gx", "gy"), split_axis=0, concat_axis=0, tiled=True),
        lax.all_to_all(send_coef, ("gx", "gy"), split_axis=0, concat_axis=0, tiled=True),
        lax.all_to_all(send_ids, ("gx", "gy"), split_axis=0, concat_axis=0, tiled=True),
    )
    my_ids = jnp.nonzero(owner == me_flat, size=SPD, fill_value=0)[0].astype(jnp.int32)
    select = (recv_ids[None, :] == my_ids[:, None]).astype(jnp.bfloat16)
    mixer = select[:, :, None] * recv_coef[None, :, :]
    obs = jnp.einsum("ksr,srp->krp", mixer, recv_rows, preferred_element_type=jnp.float32)
    owned = jnp.sum(obs * obs, axis=(1, 2)) / (foot * probe_n)
    spread = jnp.zeros((n_sens,), jnp.float32).at[my_ids].set(owned)
    sens_all = lax.psum(spread, ("gx", "gy"))
    gain = weights * jnp.sqrt(1.0 + sens_all)
    new_weights = n_sens * gain / jnp.sum(gain)
    values_pts = jnp.where(
        alive[:, None], new_weights[blk_sensor][:, None] * jnp.square(coef.astype(jnp.float32)), 0.0
    )
    density = (
        jnp.zeros((tile_r * tile_c,), jnp.float32)
        .at[blk_rows.reshape(-1)]
        .add(values_pts.reshape(-1))
    )
    return (owned, new_weights, density.reshape(tile_r, tile_c))


def solution(mesh):
    in_specs = (
        P("gx", "gy", None),
        P(("gx", "gy"), None),
        P(("gx", "gy")),
        P(("gx", "gy")),
        P(("gx", "gy"), None),
        P(),
        P(),
    )
    out_specs = (P(("gx", "gy")), P(), P("gx", "gy"))
    return jax.shard_map(local, mesh=mesh, in_specs=in_specs, out_specs=out_specs, check_vma=False)
```

profile of v0, /device:TPU:0, one launch (start us, length us, event | category | flops | bytes accessed | tf_op | source)
XLA Modules:
  0.0 216.1 jit_solution(14006273843416477223)
XLA Ops:
  0.6 0.7 compare_select_fusion.4
  2.0 1.4 gather_fusion
  3.4 0.2 convert_reduce_fusion
  3.5 0.8 scatter_custom_fusion.1
  4.4 0.7 all_to_all.16
  5.1 7.3 %all-to-all-start.1 = ((s32[32,2,1]{1,2,0:T(1,128)}), s32[32,2,1]{1,2,0:T(1,128)S(1)}, u32[]{:S(2)}, u32[]{:S(2)}) async-start(s32[32,2,1]{1,2,0:T(1,128)} %bitcast.7), calls=%async_computation.1 | async-start | bytes 32768 | tf_op jit(solution)/shard_map/all_to_all | solution.py:34
  12.4 0.7 compare_select_fusion
  13.1 1.4 scatter_custom_fusion.3
  14.5 5.1 %all-to-all-done.1 = s32[32,2,1]{1,2,0:T(1,128)S(1)} async-done(((s32[32,2,1]{1,2,0:T(1,128)}), s32[32,2,1]{1,2,0:T(1,128)S(1)}, u32[]{:S(2)}, u32[]{:S(2)}) %all-to-all-start.1) | async-done | bytes 288 | tf_op jit(solution)/shard_map/all_to_all | solution.py:34
  19.6 2.5 %all-to-all-start.2 = ((bf16[32,2,128]{2,1,0:T(2,128)(2,1)}), bf16[32,2,128]{2,1,0:T(2,128)(2,1)S(1)}, u32[]{:S(2)}, u32[]{:S(2)}) async-start(bf16[32,2,128]{2,1,0:T(2,128)(2,1)} %bitcast.13), calls=%async_computation.2 | async-start | bytes 32768 | tf_op jit(solution)/shard_map/all_to_all | solution.py:33
  22.2 15.7 %gather_fusion.1 = bf16[4096,256]{1,0:T(8,128)(2,1)S(1)} fusion(bf16[8192,256]{1,0:T(8,128)(2,1)} %bitcast.28, s32[4096]{0:T(1024)S(1)} %broadcast_clamp_fusion), kind=kCustom, calls=%fused_computation.1 | custom fusion | bytes 4210688 | tf_op jit(solution)/shard_map/gather | solution.py:19
  37.9 2.5 %broadcast_in_dim.36 = bf16[64,128,256]{2,1,0:T(8,128)(2,1)} broadcast(bf16[]{:T(256)} %constant.26.clone.1), dimensions={} | broadcast | bytes 4194306 | tf_op jit(solution)/shard_map/broadcast_in_dim | solution.py:27
  40.4 5.3 %scatter_fusion = bf16[64,128,256]{2,1,0:T(8,128)(2,1)} fusion(bf16[64,128,256]{2,1,0:T(8,128)(2,1)} %broadcast_in_dim.36, s32[32]{0:T(128)S(1)} %fusion.23, bf16[32,128,256]{2,1,0:T(8,128)(2,1)S(1)} %bitcast.29), kind=kCustom, calls=%fused_computation.3 | custom fusion | bytes 6291584 | tf_op jit(solution)/shard_map/scatter | solution.py:27
  45.7 6.3 %all-to-all-start = ((bf16[64,128,256]{2,1,0:T(8,128)(2,1)}), bf16[64,128,256]{2,1,0:T(8,128)(2,1)}, u32[]{:S(2)}, u32[]{:S(2)}) async-start(bf16[64,128,256]{2,1,0:T(8,128)(2,1)} %scatter_fusion), calls=%async_computation | async-start | bytes 8388608 | tf_op jit(solution)/shard_map/all_to_all | solution.py:32
  52.1 0.3 reduce-window.12
  52.5 0.1 slice_reduce_fusion
  52.7 2.3 %scatter_custom_fusion.2 = s32[8]{0:T(128)S(1)} fusion(s32[256]{0:T(256)S(1)} %bitcast.35, s32[256]{0:T(256)S(1)} %broadcast.233, s32[]{:T(128)} %constant.27.clone.1), kind=kCustom, calls=%fused_computation.56 | custom fusion | flops 256 | bytes 36 | tf_op jit(solution)/shard_map/scatter-add | solution.py:36
  55.0 0.2 select_n.113
  55.2 0.6 fusion.17
  55.8 0.7 compare_select_fusion.10
  56.5 0.7 fusion.20
  57.2 0.5 broadcast.255
  57.7 0.7 reduce.6
  58.7 85.6 %all-to-all-done = bf16[64,128,256]{2,1,0:T(8,128)(2,1)} async-done(((bf16[64,128,256]{2,1,0:T(8,128)(2,1)}), bf16[64,128,256]{2,1,0:T(8,128)(2,1)}, u32[]{:S(2)}, u32[]{:S(2)}) %all-to-all-start) | async-done | bytes 4194336 | tf_op jit(solution)/shard_map/all_to_all | solution.py:32
  144.2 4.6 %fusion.5 = f32[8]{0:T(128)S(1)} fusion(bf16[64,128,256]{2,1,0:T(8,128)(2,1)} %all-to-all-done, bf16[64,128]{0,1:T(8,128)(2,1)S(1)} %copy.16, bf16[8,64]{1,0:T(8,128)(2,1)S(1)} %compare_convert_fusion), kind=kOutput, calls=%fused_computation.12 | convolution fusion | flops 34144248 | bytes 4211744 | tf_op jit(solution)/shard_map/ksr,srp->krp/dot_general | solution.py:39
  148.9 0.6 scatter_custom_fusion.4
  149.5 42.0 %psum.7 = f32[256]{0:T(256)S(1)} all-reduce(f32[256]{0:T(256)S(1)} %scatter_custom_fusion.4), channel_id=1, replica_groups=mesh['gx'=8,'gy'=4] {'gx','gy'}, use_global_device_ids=true, to_apply=%region_11.12 | all-reduce | flops 256 | bytes 2048 | tf_op jit(solution)/shard_map/psum | solution.py:42
  191.5 0.6 fusion.28
  192.1 0.7 multiply_divide_fusion
  192.7 0.7 gather_fusion.2
  193.5 21.9 %scatter_custom_fusion.5 = f32[8192]{0:T(1024)S(1)} fusion(s32[4096]{0:T(1024)S(1)} %bitcast.32, f32[4096]{0:T(1024)S(1)} %select_bitcast_fusion, f32[]{:T(128)} %constant.76.clone.1), kind=kCustom, calls=%fused_computation.18 | custom fusion | flops 4096 | bytes 32772 | tf_op jit(solution)/shard_map/scatter-add | solution.py:51
  215.5 0.6 reshape.248
  (26 shorter events, 0.6 us)
Async XLA Ops:
  5.1 14.5 %all-to-all-start.1 = ((s32[32,2,1]{1,2,0:T(1,128)}), s32[32,2,1]{1,2,0:T(1,128)S(1)}, u32[]{:S(2)}, u32[]{:S(2)}) async-start(s32[32,2,1]{1,2,0:T(1,128)} %bitcast.7), calls=%async_computation.1 | async-start | bytes 32768 | tf_op jit(solution)/shard_map/all_to_all | solution.py:34
  19.6 26.1 %all-to-all-start.2 = ((bf16[32,2,128]{2,1,0:T(2,128)(2,1)}), bf16[32,2,128]{2,1,0:T(2,128)(2,1)S(1)}, u32[]{:S(2)}, u32[]{:S(2)}) async-start(bf16[32,2,128]{2,1,0:T(2,128)(2,1)} %bitcast.13), calls=%async_computation.2 | async-start | bytes 32768 | tf_op jit(solution)/shard_map/all_to_all | solution.py:33
  45.7 6.4 %copy-start = (s32[256]{0:T(256)S(1)}, s32[256]{0:T(256)}, u32[]{:S(2)}) copy-start(s32[256]{0:T(256)} %param.12) | copy-start | bytes 3076
  45.7 98.6 %all-to-all-start = ((bf16[64,128,256]{2,1,0:T(8,128)(2,1)}), bf16[64,128,256]{2,1,0:T(8,128)(2,1)}, u32[]{:S(2)}, u32[]{:S(2)}) async-start(bf16[64,128,256]{2,1,0:T(8,128)(2,1)} %scatter_fusion), calls=%async_computation | async-start | bytes 8388608 | tf_op jit(solution)/shard_map/all_to_all | solution.py:32
  52.0 139.4 %copy-start.3 = (f32[256]{0:T(256)S(1)}, f32[256]{0:T(256)}, u32[]{:S(2)}) copy-start(f32[256]{0:T(256)} %param.13) | copy-start | bytes 3076
  52.0 141.4 %copy-start.2 = (bf16[32,128]{1,0:T(8,128)(2,1)S(1)}, bf16[32,128]{1,0:T(8,128)(2,1)}, u32[]{:S(2)}) copy-start(bf16[32,128]{1,0:T(8,128)(2,1)} %param.11) | copy-start | bytes 24580
  148.8 67.2 %copy-start.4 = (f32[8]{0:T(128)}, f32[8]{0:T(128)S(1)}, u32[]{:S(2)}) copy-start(f32[8]{0:T(128)S(1)} %broadcast_multiply_fusion) | copy-start | bytes 100
  192.7 23.4 %copy-start.1 = (f32[256]{0:T(256)}, f32[256]{0:T(256)S(1)}, u32[]{:S(2)}) copy-start(f32[256]{0:T(256)S(1)} %multiply_divide_fusion) | copy-start | bytes 3076
where the time goes:
time: 217 us; the launch traced here: 216 us
  waiting for transfers between devices  90.6 us (42%)
  blocking collectives  42 us (19%)
  local copies, waits for them, and re-layouts  30.7 us (14%)
  other arithmetic  30.5 us (14%)
  starting transfers between devices  16.2 us (7%)
  matrix products  4.62 us (2%)
    all_to_all x1, waiting for transfers between devices, local(): lax.all_to_all(send_rows, ('gx', 'gy'), split_axis=0, concat_axis=0, tile...  85.6 us
    psum x1, blocking collectives, local(): sens_all = lax.psum(spread, ('gx', 'gy'))  42 us
    scatter-add x1, other arithmetic, local(): density = jnp.zeros((tile_r * tile_c,), jnp.float32).at[blk_rows.reshape(...  21.9 us
    gather x1, local copies, waits for them, and re-layouts, local(): picked = flat[blk_rows.reshape(-1)].reshape(nblk, foot, probe_n)  15.7 us
    all_to_all x1, starting transfers between devices, local(): lax.all_to_all(send_ids, ('gx', 'gy'), split_axis=0, concat_axis=0, tiled...  7.33 us
    all_to_all x1, starting transfers between devices, local(): lax.all_to_all(send_rows, ('gx', 'gy'), split_axis=0, concat_axis=0, tile...  6.35 us
    scatter x1, local copies, waits for them, and re-layouts, local(): jnp.zeros((n_dev * CAP, foot, probe_n), jnp.bfloat16).at[position]  5.29 us
    all_to_all x1, waiting for transfers between devices, local(): lax.all_to_all(send_ids, ('gx', 'gy'), split_axis=0, concat_axis=0, tiled...  5.05 us
  transfers between devices with their start and end apart: 3, of which 2 were waited for; matrix products, arithmetic and copies ran while one was open for 15% of the time, Pallas kernels for 0%

commit v1 on v0

--- a/solution.py
+++ b/solution.py
@@ -39,7 +39,9 @@
     obs = jnp.einsum("ksr,srp->krp", mixer, recv_rows, preferred_element_type=jnp.float32)
     owned = jnp.sum(obs * obs, axis=(1, 2)) / (foot * probe_n)
     spread = jnp.zeros((n_sens,), jnp.float32).at[my_ids].set(owned)
-    sens_all = lax.psum(spread, ("gx", "gy"))
+    sens_all = spread
+    for mesh_axis in ("gy", "gx"):
+        sens_all = lax.psum(sens_all, mesh_axis)
     gain = weights * jnp.sqrt(1.0 + sens_all)
     new_weights = n_sens * gain / jnp.sum(gain)
     values_pts = jnp.where(

time: 217 us -> 198 us (0.912)
  blocking collectives: 42 us -> 23.5 us
    psum x1 -> x2, blocking collectives: 42 us -> 23.5 us  [local(): sens_all = lax.psum(sens_all, mesh_axis)]
  transfers between devices with their start and end apart: 3 -> 3, of which waited for: 2 -> 2; matrix products, arithmetic and copies ran while one was open for 15% -> 16% of each run, Pallas kernels for 0% -> 0%
where the time goes in v1:
time: 198 us
  waiting for transfers between devices  90.6 us (46%)
  local copies, waits for them, and re-layouts  30.7 us (16%)
  other arithmetic  30.5 us (15%)
  blocking collectives  23.5 us (12%)
  starting transfers between devices  16.2 us (8%)
  matrix products  4.62 us (2%)
    all_to_all x1, waiting for transfers between devices, local(): lax.all_to_all(send_rows, ('gx', 'gy'), split_axis=0, concat_axis=0, tile...  85.6 us
    psum x2, blocking collectives, local(): sens_all = lax.psum(sens_all, mesh_axis)  23.5 us
    scatter-add x1, other arithmetic, local(): density = jnp.zeros((tile_r * tile_c,), jnp.float32).at[blk_rows.reshape(...  21.9 us
    gather x1, local copies, waits for them, and re-layouts, local(): picked = flat[blk_rows.reshape(-1)].reshape(nblk, foot, probe_n)  15.7 us
    all_to_all x1, starting transfers between devices, local(): lax.all_to_all(send_ids, ('gx', 'gy'), split_axis=0, concat_axis=0, tiled...  7.33 us
    all_to_all x1, starting transfers between devices, local(): lax.all_to_all(send_rows, ('gx', 'gy'), split_axis=0, concat_axis=0, tile...  6.35 us
    scatter x1, local copies, waits for them, and re-layouts, local(): jnp.zeros((n_dev * CAP, foot, probe_n), jnp.bfloat16).at[position]  5.29 us
    all_to_all x1, waiting for transfers between devices, local(): lax.all_to_all(send_ids, ('gx', 'gy'), split_axis=0, concat_axis=0, tiled...  5.05 us
  transfers between devices with their start and end apart: 3, of which 2 were waited for; matrix products, arithmetic and copies ran while one was open for 16% of the time, Pallas kernels for 0%

profile of v1, /device:TPU:0, one launch (start us, length us, event | category | flops | bytes accessed | tf_op | source)
XLA Modules:
  0.0 197.6 jit_solution(17053275645132159106)
XLA Ops:
  0.6 0.7 compare_select_fusion.4
  2.0 1.4 gather_fusion
  3.4 0.2 convert_reduce_fusion
  3.5 0.8 scatter_custom_fusion.1
  4.4 0.7 all_to_all.16
  5.1 7.3 %all-to-all-start.1 = ((s32[32,2,1]{1,2,0:T(1,128)}), s32[32,2,1]{1,2,0:T(1,128)S(1)}, u32[]{:S(2)}, u32[]{:S(2)}) async-start(s32[32,2,1]{1,2,0:T(1,128)} %bitcast.7), calls=%async_computation.1 | async-start | bytes 32768 | tf_op jit(solution)/shard_map/all_to_all | solution.py:34
  12.4 0.7 compare_select_fusion
  13.1 1.4 scatter_custom_fusion.3
  14.5 5.1 %all-to-all-done.1 = s32[32,2,1]{1,2,0:T(1,128)S(1)} async-done(((s32[32,2,1]{1,2,0:T(1,128)}), s32[32,2,1]{1,2,0:T(1,128)S(1)}, u32[]{:S(2)}, u32[]{:S(2)}) %all-to-all-start.1) | async-done | bytes 288 | tf_op jit(solution)/shard_map/all_to_all | solution.py:34
  19.6 2.5 %all-to-all-start.2 = ((bf16[32,2,128]{2,1,0:T(2,128)(2,1)}), bf16[32,2,128]{2,1,0:T(2,128)(2,1)S(1)}, u32[]{:S(2)}, u32[]{:S(2)}) async-start(bf16[32,2,128]{2,1,0:T(2,128)(2,1)} %bitcast.13), calls=%async_computation.2 | async-start | bytes 32768 | tf_op jit(solution)/shard_map/all_to_all | solution.py:33
  22.2 15.7 %gather_fusion.1 = bf16[4096,256]{1,0:T(8,128)(2,1)S(1)} fusion(bf16[8192,256]{1,0:T(8,128)(2,1)} %bitcast.28, s32[4096]{0:T(1024)S(1)} %broadcast_clamp_fusion), kind=kCustom, calls=%fused_computation.1 | custom fusion | bytes 4210688 | tf_op jit(solution)/shard_map/gather | solution.py:19
  37.9 2.5 %broadcast_in_dim.36 = bf16[64,128,256]{2,1,0:T(8,128)(2,1)} broadcast(bf16[]{:T(256)} %constant.26.clone.1), dimensions={} | broadcast | bytes 4194306 | tf_op jit(solution)/shard_map/broadcast_in_dim | solution.py:27
  40.4 5.3 %scatter_fusion = bf16[64,128,256]{2,1,0:T(8,128)(2,1)} fusion(bf16[64,128,256]{2,1,0:T(8,128)(2,1)} %broadcast_in_dim.36, s32[32]{0:T(128)S(1)} %fusion.23, bf16[32,128,256]{2,1,0:T(8,128)(2,1)S(1)} %bitcast.29), kind=kCustom, calls=%fused_computation.3 | custom fusion | bytes 6291584 | tf_op jit(solution)/shard_map/scatter | solution.py:27
  45.7 6.3 %all-to-all-start = ((bf16[64,128,256]{2,1,0:T(8,128)(2,1)}), bf16[64,128,256]{2,1,0:T(8,128)(2,1)}, u32[]{:S(2)}, u32[]{:S(2)}) async-start(bf16[64,128,256]{2,1,0:T(8,128)(2,1)} %scatter_fusion), calls=%async_computation | async-start | bytes 8388608 | tf_op jit(solution)/shard_map/all_to_all | solution.py:32
  52.1 0.3 reduce-window.12
  52.7 2.3 %scatter_custom_fusion.2 = s32[8]{0:T(128)S(1)} fusion(s32[256]{0:T(256)S(1)} %bitcast.35, s32[256]{0:T(256)S(1)} %broadcast.233, s32[]{:T(128)} %constant.27.clone.1), kind=kCustom, calls=%fused_computation.56 | custom fusion | flops 256 | bytes 36 | tf_op jit(solution)/shard_map/scatter-add | solution.py:36
  55.0 0.2 select_n.113
  55.2 0.6 fusion.17
  55.8 0.7 compare_select_fusion.10
  56.5 0.7 fusion.20
  57.2 0.5 broadcast.255
  57.7 0.7 reduce.6
  58.7 85.6 %all-to-all-done = bf16[64,128,256]{2,1,0:T(8,128)(2,1)} async-done(((bf16[64,128,256]{2,1,0:T(8,128)(2,1)}), bf16[64,128,256]{2,1,0:T(8,128)(2,1)}, u32[]{:S(2)}, u32[]{:S(2)}) %all-to-all-start) | async-done | bytes 4194336 | tf_op jit(solution)/shard_map/all_to_all | solution.py:32
  144.2 4.6 %fusion.5 = f32[8]{0:T(128)S(1)} fusion(bf16[64,128,256]{2,1,0:T(8,128)(2,1)} %all-to-all-done, bf16[64,128]{0,1:T(8,128)(2,1)S(1)} %copy.16, bf16[8,64]{1,0:T(8,128)(2,1)S(1)} %compare_convert_fusion), kind=kOutput, calls=%fused_computation.12 | convolution fusion | flops 34144248 | bytes 4211744 | tf_op jit(solution)/shard_map/ksr,srp->krp/dot_general | solution.py:39
  148.9 0.6 scatter_custom_fusion.4
  149.5 11.7 %psum.14 = f32[256]{0:T(256)S(1)} all-reduce(f32[256]{0:T(256)S(1)} %scatter_custom_fusion.4), channel_id=1, replica_groups=mesh['gx'=8,'gy'=4] {'gy'}, use_global_device_ids=true, to_apply=%region_11.12 | all-reduce | flops 256 | bytes 2048 | tf_op jit(solution)/shard_map/psum | solution.py:44
  161.2 11.8 %psum.15 = f32[256]{0:T(256)S(1)} all-reduce(f32[256]{0:T(256)S(1)} %psum.14), channel_id=1, replica_groups=mesh['gx'=8,'gy'=4] {'gx'}, use_global_device_ids=true, to_apply=%region_12.13 | all-reduce | flops 256 | bytes 2048 | tf_op jit(solution)/shard_map/psum | solution.py:44
  173.0 0.6 fusion.28
  173.6 0.7 multiply_divide_fusion
  174.3 0.7 gather_fusion.2
  175.0 21.9 %scatter_custom_fusion.5 = f32[8192]{0:T(1024)S(1)} fusion(s32[4096]{0:T(1024)S(1)} %bitcast.32, f32[4096]{0:T(1024)S(1)} %select_bitcast_fusion, f32[]{:T(128)} %constant.76.clone.1), kind=kCustom, calls=%fused_computation.18 | custom fusion | flops 4096 | bytes 32772 | tf_op jit(solution)/shard_map/scatter-add | solution.py:53
  197.0 0.6 reshape.248
  (27 shorter events, 0.7 us)
Async XLA Ops:
  5.1 14.5 %all-to-all-start.1 = ((s32[32,2,1]{1,2,0:T(1,128)}), s32[32,2,1]{1,2,0:T(1,128)S(1)}, u32[]{:S(2)}, u32[]{:S(2)}) async-start(s32[32,2,1]{1,2,0:T(1,128)} %bitcast.7), calls=%async_computation.1 | async-start | bytes 32768 | tf_op jit(solution)/shard_map/all_to_all | solution.py:34
  19.6 26.1 %all-to-all-start.2 = ((bf16[32,2,128]{2,1,0:T(2,128)(2,1)}), bf16[32,2,128]{2,1,0:T(2,128)(2,1)S(1)}, u32[]{:S(2)}, u32[]{:S(2)}) async-start(bf16[32,2,128]{2,1,0:T(2,128)(2,1)} %bitcast.13), calls=%async_computation.2 | async-start | bytes 32768 | tf_op jit(solution)/shard_map/all_to_all | solution.py:33
  45.7 6.4 %copy-start = (s32[256]{0:T(256)S(1)}, s32[256]{0:T(256)}, u32[]{:S(2)}) copy-start(s32[256]{0:T(256)} %param.12) | copy-start | bytes 3076
  45.7 98.6 %all-to-all-start = ((bf16[64,128,256]{2,1,0:T(8,128)(2,1)}), bf16[64,128,256]{2,1,0:T(8,128)(2,1)}, u32[]{:S(2)}, u32[]{:S(2)}) async-start(bf16[64,128,256]{2,1,0:T(8,128)(2,1)} %scatter_fusion), calls=%async_computation | async-start | bytes 8388608 | tf_op jit(solution)/shard_map/all_to_all | solution.py:32
  52.0 121.0 %copy-start.3 = (f32[256]{0:T(256)S(1)}, f32[256]{0:T(256)}, u32[]{:S(2)}) copy-start(f32[256]{0:T(256)} %param.13) | copy-start | bytes 3076
  52.0 122.9 %copy-start.2 = (bf16[32,128]{1,0:T(8,128)(2,1)S(1)}, bf16[32,128]{1,0:T(8,128)(2,1)}, u32[]{:S(2)}) copy-start(bf16[32,128]{1,0:T(8,128)(2,1)} %param.11) | copy-start | bytes 24580
  148.8 48.8 %copy-start.4 = (f32[8]{0:T(128)}, f32[8]{0:T(128)S(1)}, u32[]{:S(2)}) copy-start(f32[8]{0:T(128)S(1)} %broadcast_multiply_fusion) | copy-start | bytes 100
  174.2 23.4 %copy-start.1 = (f32[256]{0:T(256)}, f32[256]{0:T(256)S(1)}, u32[]{:S(2)}) copy-start(f32[256]{0:T(256)S(1)} %multiply_divide_fusion) | copy-start | bytes 3076
